TPU v7x, 32 devices: a whole 2x2x4 slice. The times are simulated.
32 devices in a mesh: tensor: 2 (over y), dp: 4 (over x, core), seq: 4 (over z).
Axes of the slice: x: 2, y: 2, z: 4, core: 2. Of those that a mesh axis runs over, the one named last changes fastest.
Arguments:
- tokens: bfloat16 [8, 1024, 2048], P('dp', 'seq'), may hold values from -6 to 6
- ln1_gain: bfloat16 [2048], P(('dp', 'seq')), may hold values from 0.5 to 1.5
- ln1_bias: bfloat16 [2048], P(('dp', 'seq')), may hold values from -3 to 3
- ln2_gain: bfloat16 [2048], P(('dp', 'seq')), may hold values from 0.5 to 1.5
- ln2_bias: bfloat16 [2048], P(('dp', 'seq')), may hold values from -3 to 3
- w_query: bfloat16 [2048, 2048], P(('dp', 'seq'), 'tensor'), may hold values from -0.125 to 0.125
- w_key: bfloat16 [2048, 2048], P(('dp', 'seq'), 'tensor'), may hold values from -0.125 to 0.125
- w_value: bfloat16 [2048, 4096], P(('dp', 'seq'), 'tensor'), may hold values from -0.125 to 0.125
- w_swish: bfloat16 [2048, 4096], P(('dp', 'seq'), 'tensor'), may hold values from -0.125 to 0.125
- w_out: bfloat16 [4096, 2048], P('tensor', ('dp', 'seq')), may hold values from -0.1875 to 0.1875
- w_gate: bfloat16 [2048, 4096], P(('dp', 'seq'), 'tensor'), may hold values from -0.125 to 0.125
- w_up: bfloat16 [2048, 4096], P(('dp', 'seq'), 'tensor'), may hold values from -0.125 to 0.125
- w_down: bfloat16 [4096, 2048], P('tensor', ('dp', 'seq')), may hold values from -0.09375 to 0.09375
- decay_rate: float32 [8], P('tensor'), may hold values from 0 to 1, as said below
- cotangent: bfloat16 [8, 1024, 2048], P('dp', 'seq'), may hold values from -6 to 6
Outputs:
- mixed_out: bfloat16 [8, 1024, 2048], P('dp', 'seq')
- input_grad: float32 [8, 1024, 2048], P('dp', 'seq')
- ln1_gain_grad: float32 [2048], P(('dp', 'seq'))
- ln1_bias_grad: float32 [2048], P(('dp', 'seq'))
- ln2_gain_grad: float32 [2048], P(('dp', 'seq'))
- ln2_bias_grad: float32 [2048], P(('dp', 'seq'))
- w_query_grad: float32 [2048, 2048], P(('dp', 'seq'), 'tensor')
- w_key_grad: float32 [2048, 2048], P(('dp', 'seq'), 'tensor')
- w_value_grad: float32 [2048, 4096], P(('dp', 'seq'), 'tensor')
- w_swish_grad: float32 [2048, 4096], P(('dp', 'seq'), 'tensor')
- w_out_grad: float32 [4096, 2048], P('tensor', ('dp', 'seq'))
- w_gate_grad: float32 [2048, 4096], P(('dp', 'seq'), 'tensor')
- w_up_grad: float32 [2048, 4096], P(('dp', 'seq'), 'tensor')
- w_down_grad: float32 [4096, 2048], P('tensor', ('dp', 'seq'))
Inputs may be any that keep to these rules, and one draw needn't show every extreme that they name: `decay_rate`: each head's rate lies between 0.3 / 1024 and 1 / 30.
All inputs are finite; a program needn't handle non-finite values.
Results may differ from a plain program's by a relative error of at most 0.014.
Values may be sent and summed in bfloat16 or wider, within the bound.
A program may use at most 256 MiB of HBM per device.

v0:
```python
import jax
import jax.numpy as jnp
from jax import lax
from jax.sharding import PartitionSpec as P

KD = 256
VH = 512
eps = 1e-05
highest_precision = lax.Precision.HIGHEST


def passed_along(x, axis, by):
    count = lax.axis_size(axis)
    pairs = [(i, i + by) for i in range(count) if 0 <= i + by < count]
    return lax.ppermute(x, axis, pairs)


def normalize(values):
    centred = values - jnp.mean(values, axis=-1, keepdims=True)
    spread = jnp.mean(centred * centred, axis=-1, keepdims=True)
    scaling = lax.rsqrt(spread + eps)
    return (centred * scaling, scaling)


def norm_back(grad_normed, normed, scaling):
    first_mean = jnp.mean(grad_normed, axis=-1, keepdims=True)
    second_mean = jnp.mean(grad_normed * normed, axis=-1, keepdims=True)
    return scaling * (grad_normed - first_mean - normed * second_mean)


def turn_angles(positions, half_width):
    frequency = 10000.0 ** (-jnp.arange(half_width, dtype=jnp.float32) / max(half_width - 1, 1))
    angles = positions[:, None] * frequency[None, :]
    return (jnp.cos(angles)[:, None, :], jnp.sin(angles)[:, None, :])


def rotate(values, cosine, sine_table):
    half_width = values.shape[-1] // 2
    first_half = values[..., :half_width]
    second_half = values[..., half_width:]
    return jnp.concatenate(
        [
            first_half * cosine - second_half * sine_table,
            second_half * cosine + first_half * sine_table,
        ],
        axis=-1,
    )


def decay_tables(decay_rate, block):
    places = jnp.arange(block, dtype=jnp.float32)
    distance = places[:, None] - places[None, :]
    inside = jnp.where(
        distance[None] >= 0.0,
        jnp.exp(-decay_rate[:, None, None] * jnp.maximum(distance, 0.0)[None]),
        0.0,
    )
    query_decay_factor = jnp.exp(-decay_rate[None, :] * (places[:, None] + 1.0))[..., None]
    key_decay_factor = jnp.exp(-decay_rate[None, :] * (block - 1.0 - places[:, None]))[..., None]
    block_decay_factor = jnp.exp(-decay_rate * block)[:, None, None]
    return (inside, query_decay_factor, key_decay_factor, block_decay_factor)


def matmul(left, right):
    return jnp.dot(left, right, preferred_element_type=jnp.float32)


def on_device(
    tokens,
    ln1_gain,
    ln1_bias,
    ln2_gain,
    ln2_bias,
    w_query,
    w_key,
    w_value,
    w_swish,
    w_out,
    w_gate,
    w_up,
    w_down,
    decay_rate,
    cotangent,
):
    gathered = (
        lax.all_gather(ln1_gain, ("dp", "seq"), axis=0, tiled=True),
        lax.all_gather(ln1_bias, ("dp", "seq"), axis=0, tiled=True),
        lax.all_gather(ln2_gain, ("dp", "seq"), axis=0, tiled=True),
        lax.all_gather(ln2_bias, ("dp", "seq"), axis=0, tiled=True),
        lax.all_gather(w_query, ("dp", "seq"), axis=0, tiled=True),
        lax.all_gather(w_key, ("dp", "seq"), axis=0, tiled=True),
        lax.all_gather(w_value, ("dp", "seq"), axis=0, tiled=True),
        lax.all_gather(w_swish, ("dp", "seq"), axis=0, tiled=True),
        lax.all_gather(w_gate, ("dp", "seq"), axis=0, tiled=True),
        lax.all_gather(w_up, ("dp", "seq"), axis=0, tiled=True),
    )
    norm_gain = gathered[0].astype(jnp.float32)
    norm_bias = gathered[1].astype(jnp.float32)
    mlp_gain = gathered[2].astype(jnp.float32)
    mlp_bias = gathered[3].astype(jnp.float32)
    query_full, key_full, value_full, swish_full, gate_full, up_full = gathered[4:]
    out_full, down_full = (
        lax.all_gather(w_out, ("dp", "seq"), axis=1, tiled=True),
        lax.all_gather(w_down, ("dp", "seq"), axis=1, tiled=True),
    )
    seq_count, block, width = tokens.shape
    row_count = seq_count * block
    heads = decay_rate.shape[0]
    inputs = tokens.astype(jnp.float32).reshape(row_count, width)
    normed_one, scale_one = normalize(inputs)
    first = (normed_one * norm_gain + norm_bias).astype(jnp.bfloat16)
    queries = matmul(first, query_full).reshape(seq_count, block, heads, KD)
    keys_lin = matmul(first, key_full).reshape(seq_count, block, heads, KD)
    value_rows = matmul(first, value_full).astype(jnp.bfloat16).reshape(seq_count, block, heads, VH)
    gate_pre = matmul(first, swish_full)
    offset = lax.axis_index("seq") * block
    positions = (offset + jnp.arange(block, dtype=jnp.int32)).astype(jnp.float32)
    cosine, sine_table = turn_angles(positions, KD // 2)
    query_rot = rotate(queries, cosine, sine_table).astype(jnp.bfloat16)
    key_rot = rotate(keys_lin, cosine, sine_table).astype(jnp.bfloat16)
    inside, query_decay_factor, key_decay_factor, block_decay_factor = decay_tables(
        decay_rate, block
    )
    scores = jnp.einsum("snhk,smhk->shnm", query_rot, key_rot, preferred_element_type=jnp.float32)
    weights = (scores * inside).astype(jnp.bfloat16)
    within = jnp.einsum("shnm,smhv->snhv", weights, value_rows, preferred_element_type=jnp.float32)
    query_scaled = query_rot.astype(jnp.float32) * query_decay_factor
    key_scaled = key_rot.astype(jnp.float32) * key_decay_factor
    value_wide = value_rows.astype(jnp.float32)
    local_state = jnp.einsum("smhk,smhv->shkv", key_scaled, value_wide, precision=highest_precision)

    def pass_state(turn, carry):
        incoming = passed_along(carry[1], "seq", 1)
        return (incoming, block_decay_factor * incoming + local_state)

    state_in = lax.fori_loop(
        0, lax.axis_size("seq") - 1, pass_state, (jnp.zeros_like(local_state), local_state)
    )[0]
    cross_block_term = jnp.einsum(
        "snhk,shkv->snhv", query_scaled, state_in, precision=highest_precision
    )
    retained = within + cross_block_term
    group_normed, group_scale = normalize(retained)
    group_flat = group_normed.reshape(row_count, heads * VH)
    gate_act, swish_pull = jax.vjp(jax.nn.silu, gate_pre)
    mixed = (gate_act * group_flat).astype(jnp.bfloat16)
    attention = lax.psum(matmul(mixed, out_full), "tensor")
    hidden_in = inputs + attention
    normed_two, scale_two = normalize(hidden_in)
    second = (normed_two * mlp_gain + mlp_bias).astype(jnp.bfloat16)
    gate_lin = matmul(second, gate_full)
    up_lin = matmul(second, up_full)
    gate_gelu, gelu_pull = jax.vjp(jax.nn.gelu, gate_lin)
    hidden = (gate_gelu * up_lin).astype(jnp.bfloat16)
    feed = lax.psum(matmul(hidden, down_full).astype(jnp.bfloat16), "tensor").astype(jnp.float32)
    mixed_out = (hidden_in + feed).astype(jnp.bfloat16).reshape(seq_count, block, width)
    grad_rows = cotangent.reshape(row_count, width)
    grad_down = jnp.einsum("rf,rd->fd", hidden, grad_rows, preferred_element_type=jnp.float32)
    grad_hidden = jnp.einsum("rd,fd->rf", grad_rows, down_full, preferred_element_type=jnp.float32)
    grad_gate_lin = gelu_pull(grad_hidden * up_lin)[0].astype(jnp.bfloat16)
    grad_up_lin = (grad_hidden * gate_gelu).astype(jnp.bfloat16)
    grad_gate = jnp.einsum("rd,rf->df", second, grad_gate_lin, preferred_element_type=jnp.float32)
    grad_up = jnp.einsum("rd,rf->df", second, grad_up_lin, preferred_element_type=jnp.float32)
    second_part = jnp.einsum(
        "rf,df->rd", grad_gate_lin, gate_full, preferred_element_type=jnp.float32
    )
    second_part = second_part + jnp.einsum(
        "rf,df->rd", grad_up_lin, up_full, preferred_element_type=jnp.float32
    )
    grad_second = lax.psum(second_part, "tensor")
    grad_mlp_gain = jnp.sum(grad_second * normed_two, axis=0)
    grad_mlp_bias = jnp.sum(grad_second, axis=0)
    grad_hidden_in = grad_rows.astype(jnp.float32) + norm_back(
        grad_second * mlp_gain, normed_two, scale_two
    )
    grad_branch = grad_hidden_in.astype(jnp.bfloat16)
    grad_out_w = jnp.einsum("rv,rd->vd", mixed, grad_branch, preferred_element_type=jnp.float32)
    grad_mixed = jnp.einsum("rd,vd->rv", grad_branch, out_full, preferred_element_type=jnp.float32)
    grad_gate_pre = swish_pull(grad_mixed * group_flat)[0].astype(jnp.bfloat16)
    grad_group = (grad_mixed * gate_act).reshape(seq_count, block, heads, VH)
    grad_retained = norm_back(grad_group, group_normed, group_scale).astype(jnp.bfloat16)
    grad_weights = jnp.einsum(
        "snhv,smhv->shnm", grad_retained, value_rows, preferred_element_type=jnp.float32
    )
    grad_scores = (grad_weights * inside).astype(jnp.bfloat16)
    grad_query = jnp.einsum(
        "shnm,smhk->snhk", grad_scores, key_rot, preferred_element_type=jnp.float32
    )
    grad_key = jnp.einsum(
        "shnm,snhk->smhk", grad_scores, query_rot, preferred_element_type=jnp.float32
    )
    grad_value = jnp.einsum(
        "shnm,snhv->smhv", weights, grad_retained, preferred_element_type=jnp.float32
    )
    grad_wide = grad_retained.astype(jnp.float32)
    grad_query = grad_query + query_decay_factor * jnp.einsum(
        "snhv,shkv->snhk", grad_wide, state_in, precision=highest_precision
    )
    local_grad = jnp.einsum("snhk,snhv->shkv", query_scaled, grad_wide, precision=highest_precision)

    def pass_grad(turn, carry):
        incoming = passed_along(carry[1], "seq", -1)
        return (incoming, block_decay_factor * incoming + local_grad)

    state_grad = lax.fori_loop(
        0, lax.axis_size("seq") - 1, pass_grad, (jnp.zeros_like(local_grad), local_grad)
    )[0]
    grad_key = grad_key + key_decay_factor * jnp.einsum(
        "smhv,shkv->smhk", value_wide, state_grad, precision=highest_precision
    )
    grad_value = grad_value + jnp.einsum(
        "smhk,shkv->smhv", key_scaled, state_grad, precision=highest_precision
    )
    grad_query_pre = (
        rotate(grad_query, cosine, -sine_table).reshape(row_count, heads * KD).astype(jnp.bfloat16)
    )
    grad_key_pre = (
        rotate(grad_key, cosine, -sine_table).reshape(row_count, heads * KD).astype(jnp.bfloat16)
    )
    grad_value_pre = grad_value.reshape(row_count, heads * VH).astype(jnp.bfloat16)
    grad_wq = jnp.einsum("rd,rk->dk", first, grad_query_pre, preferred_element_type=jnp.float32)
    grad_wk = jnp.einsum("rd,rk->dk", first, grad_key_pre, preferred_element_type=jnp.float32)
    grad_wv = jnp.einsum("rd,rk->dk", first, grad_value_pre, preferred_element_type=jnp.float32)
    grad_ws = jnp.einsum("rd,rk->dk", first, grad_gate_pre, preferred_element_type=jnp.float32)
    first_part = jnp.einsum(
        "rk,dk->rd", grad_query_pre, query_full, preferred_element_type=jnp.float32
    )
    first_part = first_part + jnp.einsum(
        "rk,dk->rd", grad_key_pre, key_full, preferred_element_type=jnp.float32
    )
    first_part = first_part + jnp.einsum(
        "rk,dk->rd", grad_value_pre, value_full, preferred_element_type=jnp.float32
    )
    first_part = first_part + jnp.einsum(
        "rk,dk->rd", grad_gate_pre, swish_full, preferred_element_type=jnp.float32
    )
    grad_first = lax.psum(first_part, "tensor")
    grad_norm_gain = jnp.sum(grad_first * normed_one, axis=0)
    grad_norm_bias = jnp.sum(grad_first, axis=0)
    grad_inputs = grad_hidden_in + norm_back(grad_first * norm_gain, normed_one, scale_one)
    input_grad = grad_inputs.reshape(seq_count, block, width)
    row_sums = (
        lax.psum_scatter(grad_out_w, ("dp", "seq"), scatter_dimension=1, tiled=True),
        lax.psum_scatter(grad_down, ("dp", "seq"), scatter_dimension=1, tiled=True),
    )
    column_sums = (
        lax.psum_scatter(grad_norm_gain, ("dp", "seq"), scatter_dimension=0, tiled=True),
        lax.psum_scatter(grad_norm_bias, ("dp", "seq"), scatter_dimension=0, tiled=True),
        lax.psum_scatter(grad_mlp_gain, ("dp", "seq"), scatter_dimension=0, tiled=True),
        lax.psum_scatter(grad_mlp_bias, ("dp", "seq"), scatter_dimension=0, tiled=True),
        lax.psum_scatter(grad_wq, ("dp", "seq"), scatter_dimension=0, tiled=True),
        lax.psum_scatter(grad_wk, ("dp", "seq"), scatter_dimension=0, tiled=True),
        lax.psum_scatter(grad_wv, ("dp", "seq"), scatter_dimension=0, tiled=True),
        lax.psum_scatter(grad_ws, ("dp", "seq"), scatter_dimension=0, tiled=True),
        lax.psum_scatter(grad_gate, ("dp", "seq"), scatter_dimension=0, tiled=True),
        lax.psum_scatter(grad_up, ("dp", "seq"), scatter_dimension=0, tiled=True),
    )
    return (
        mixed_out,
        input_grad,
        column_sums[0],
        column_sums[1],
        column_sums[2],
        column_sums[3],
        column_sums[4],
        column_sums[5],
        column_sums[6],
        column_sums[7],
        row_sums[0],
        column_sums[8],
        column_sums[9],
        row_sums[1],
    )


def solution(mesh):
    return jax.shard_map(
        on_device,
        mesh=mesh,
        in_specs=(
            P("dp", "seq", None),
            P(("dp", "seq")),
            P(("dp", "seq")),
            P(("dp", "seq")),
            P(("dp", "seq")),
            P(("dp", "seq"), "tensor"),
            P(("dp", "seq"), "tensor"),
            P(("dp", "seq"), "tensor"),
            P(("dp", "seq"), "tensor"),
            P("tensor", ("dp", "seq")),
            P(("dp", "seq"), "tensor"),
            P(("dp", "seq"), "tensor"),
            P("tensor", ("dp", "seq")),
            P("tensor"),
            P("dp", "seq", None),
        ),
        out_specs=(
            P("dp", "seq", None),
            P("dp", "seq", None),
            P(("dp", "seq")),
            P(("dp", "seq")),
            P(("dp", "seq")),
            P(("dp", "seq")),
            P(("dp", "seq"), "tensor"),
            P(("dp", "seq"), "tensor"),
            P(("dp", "seq"), "tensor"),
            P(("dp", "seq"), "tensor"),
            P("tensor", ("dp", "seq")),
            P(("dp", "seq"), "tensor"),
            P(("dp", "seq"), "tensor"),
            P("tensor", ("dp", "seq")),
        ),
        check_vma=False,
    )
```

profile of v0, /device:TPU:0, one launch (start us, length us, event | category | flops | bytes accessed | tf_op | source)
XLA Modules:
  0.0 3024.8 jit_solution(7418860865744071854)
XLA Ops:
  10.6 34.2 %all-gather = bf16[16,1,128]{2,1,0:T(2,128)(2,1)S(1)} all-gather(bf16[1,1,128]{2,1,0:T(2,128)(2,1)} %bitcast.195), channel_id=1, replica_groups=mesh['tensor'=2,'dp'=4,'seq'=4] {'dp','seq'}, dimensions={0}, use_global_device_ids=true | all-gather | bytes 4352 | tf_op jit(solution)/shard_map/all_gather | solution.py:86
  44.8 29.1 all-gather.1
  89.8 24.9 all-gather.17.cloned.1.call-done
  132.7 57.1 %all-gather.15.cloned.1.call-done = bf16[2048,2048]{1,0:T(8,128)(2,1)} async-done(((bf16[128,2048]{1,0:T(8,128)(2,1)}), bf16[2048,2048]{1,0:T(8,128)(2,1)}) %all-gather.15.cloned.1.call-update) | async-done | bytes 8388624 | tf_op jit(solution)/shard_map/all_gather | solution.py:92
  189.8 9.8 convolution_convert_fusion.1
  214.2 374.2 %while.24 = (s32[]{:T(128)}, f32[2,4,256,512]{3,2,1,0:T(8,128)}, f32[2,4,256,512]{3,2,1,0:T(8,128)}, f32[4]{0:T(128)S(1)}, f32[2,4,256,512]{3,2,1,0:T(8,128)}, /*index=5*/s32[]{:T(128)}) while((s32[]{:T(128)}, f32[2,4,256,512]{3,2,1,0:T(8,128)}, f32[2,4,256,512]{3,2,1,0:T(8,128)}, f32[4]{0:T(128)S(1)}, f32[2,4,256,512]{3,2,1,0:T(8,128)}, ...), condition=%wide.region_3.4_spmd, body=%wide.region_2.3_spmd.sunk | while | flops 2097154 | bytes 29360252 | solution.py:136
  219.7 154.2 %collective-permute-done = f32[2,4,256,512]{3,2,1,0:T(8,128)} collective-permute-done((f32[2,4,256,512]{3,2,1,0:T(8,128)}, f32[2,4,256,512]{3,2,1,0:T(8,128)}, u32[]{:S(2)}, u32[]{:S(2)}) %collective-permute-start) | collective-permute-done | bytes 4194336 | tf_op jit(solution)/shard_map/while/body/eval_jaxpr/ppermute | solution.py:15
  380.5 9.6 collective-permute-start
  390.0 92.2 %collective-permute-done = f32[2,4,256,512]{3,2,1,0:T(8,128)} collective-permute-done((f32[2,4,256,512]{3,2,1,0:T(8,128)}, f32[2,4,256,512]{3,2,1,0:T(8,128)}, u32[]{:S(2)}, u32[]{:S(2)}) %collective-permute-start) | collective-permute-done | bytes 4194336 | tf_op jit(solution)/shard_map/while/body/eval_jaxpr/ppermute | solution.py:15
  495.3 86.5 %collective-permute-done = f32[2,4,256,512]{3,2,1,0:T(8,128)} collective-permute-done((f32[2,4,256,512]{3,2,1,0:T(8,128)}, f32[2,4,256,512]{3,2,1,0:T(8,128)}, u32[]{:S(2)}, u32[]{:S(2)}) %collective-permute-start) | collective-permute-done | bytes 4194336 | tf_op jit(solution)/shard_map/while/body/eval_jaxpr/ppermute | solution.py:15
  614.8 12.9 multiply_convert_fusion.3
  627.6 10.5 fusion.62
  640.4 32.5 %all-gather.2 = bf16[16,1,128]{2,1,0:T(2,128)(2,1)S(1)} all-gather(bf16[1,1,128]{2,1,0:T(2,128)(2,1)S(1)} %bitcast.197), channel_id=1, replica_groups=mesh['tensor'=2,'dp'=4,'seq'=4] {'dp','seq'}, dimensions={0}, use_global_device_ids=true | all-gather | bytes 4352 | tf_op jit(solution)/shard_map/all_gather | solution.py:88
  673.0 28.5 all-gather.3
  701.4 46.9 %all-reduce.10.cloned.1.call-done = f32[512,2048]{1,0:T(8,128)} async-done(((f32[512,2048]{1,0:T(8,128)}), f32[512,2048]{1,0:T(8,128)}) %all-reduce.10.cloned.1.call-update) | async-done | bytes 4194320 | tf_op jit(solution)/shard_map/psum | solution.py:147
  753.9 71.0 %all-gather.23.cloned.1.call-done = bf16[2048,2048]{1,0:T(8,128)(2,1)} async-done(((bf16[128,2048]{1,0:T(8,128)(2,1)}), bf16[2048,2048]{1,0:T(8,128)(2,1)}) %all-gather.23.cloned.1.call-update) | async-done | bytes 8388624 | tf_op jit(solution)/shard_map/all_gather | solution.py:94
  824.9 9.8 fusion.63
  834.7 65.3 %all-gather.25.cloned.1.call-done = bf16[2048,2048]{1,0:T(8,128)(2,1)} async-done(((bf16[128,2048]{1,0:T(8,128)(2,1)}), bf16[2048,2048]{1,0:T(8,128)(2,1)}) %all-gather.25.cloned.1.call-update) | async-done | bytes 8388624 | tf_op jit(solution)/shard_map/all_gather | solution.py:95
  900.0 9.4 fusion.64
  909.4 69.0 %all-gather.27.cloned.1.call-done = bf16[2048,2048]{1,0:T(8,128)(2,1)} async-done(((bf16[2048,128]{1,0:T(8,128)(2,1)}), bf16[2048,2048]{1,0:T(8,128)(2,1)}) %all-gather.27.cloned.1.call-update) | async-done | bytes 8388624 | tf_op jit(solution)/shard_map/all_gather | solution.py:104
  978.4 12.2 multiply_convert_fusion.1
  990.7 9.2 fusion.65
  1006.2 9.2 convolution_convert_fusion
  1015.5 96.9 %all-reduce.14.cloned.1.call-done = f32[512,2048]{1,0:T(8,128)} async-done(((f32[512,2048]{1,0:T(8,128)}), f32[512,2048]{1,0:T(8,128)}) %all-reduce.14.cloned.1.call-update) | async-done | bytes 4194320 | tf_op jit(solution)/shard_map/psum | solution.py:170
  1117.4 60.9 %all-reduce.12.cloned.1.call-done = bf16[512,2048]{1,0:T(8,128)(2,1)} async-done(((bf16[512,2048]{1,0:T(8,128)(2,1)}), bf16[512,2048]{1,0:T(8,128)(2,1)}) %all-reduce.12.cloned.1.call-update) | async-done | bytes 2097168 | tf_op jit(solution)/shard_map/psum | solution.py:155
  1185.0 13.5 fusion.9
  1239.9 300.7 %while.25 = (s32[]{:T(128)}, f32[2,4,256,512]{3,2,1,0:T(8,128)}, f32[2,4,256,512]{3,2,1,0:T(8,128)}, f32[4]{0:T(128)S(1)}, f32[2,4,256,512]{3,2,1,0:T(8,128)}, /*index=5*/s32[]{:T(128)}) while((s32[]{:T(128)}, f32[2,4,256,512]{3,2,1,0:T(8,128)}, f32[2,4,256,512]{3,2,1,0:T(8,128)}, f32[4]{0:T(128)S(1)}, f32[2,4,256,512]{3,2,1,0:T(8,128)}, ...), condition=%wide.region_16.17_spmd, body=%wide.region_15.16_spmd.sunk | while | flops 2097154 | bytes 29360252 | solution.py:205
  1241.3 93.1 %collective-permute-done.1 = f32[2,4,256,512]{3,2,1,0:T(8,128)} collective-permute-done((f32[2,4,256,512]{3,2,1,0:T(8,128)}, f32[2,4,256,512]{3,2,1,0:T(8,128)}, u32[]{:S(2)}, u32[]{:S(2)}) %collective-permute-start.1) | collective-permute-done | bytes 4194336 | tf_op jit(solution)/shard_map/while/body/eval_jaxpr/ppermute | solution.py:15
  1342.2 92.2 %collective-permute-done.1 = f32[2,4,256,512]{3,2,1,0:T(8,128)} collective-permute-done((f32[2,4,256,512]{3,2,1,0:T(8,128)}, f32[2,4,256,512]{3,2,1,0:T(8,128)}, u32[]{:S(2)}, u32[]{:S(2)}) %collective-permute-start.1) | collective-permute-done | bytes 4194336 | tf_op jit(solution)/shard_map/while/body/eval_jaxpr/ppermute | solution.py:15
  1442.3 91.3 %collective-permute-done.1 = f32[2,4,256,512]{3,2,1,0:T(8,128)} collective-permute-done((f32[2,4,256,512]{3,2,1,0:T(8,128)}, f32[2,4,256,512]{3,2,1,0:T(8,128)}, u32[]{:S(2)}, u32[]{:S(2)}) %collective-permute-start.1) | collective-permute-done | bytes 4194336 | tf_op jit(solution)/shard_map/while/body/eval_jaxpr/ppermute | solution.py:15
  1540.6 11.1 fusion.38
  1596.3 11.2 add_add_fusion
  1621.9 12.6 fusion.73
  1634.6 12.5 fusion.74
  1647.7 12.6 fusion.75
  1660.3 13.4 fusion.45
  1673.8 10.1 fusion.71
  1685.5 10.0 fusion.72
  1697.4 17.2 all-reduce.16.cloned.1.call-done
  1718.3 63.8 %all-reduce.4 = (f32[2048]{0:T(1024)S(1)}, f32[2048]{0:T(1024)S(1)}, f32[2048]{0:T(1024)S(1)}, f32[2048]{0:T(1024)S(1)}) all-reduce(f32[2048]{0:T(1024)S(1)} %get-tuple-element.70, f32[2048]{0:T(1024)S(1)} %get-tuple-element.75, f32[2048]{0:T(1024)S(1)} %copy-done.52, ...), channel_id=2, replica_groups=mesh['tensor'=2,'dp'=4,'seq'=4] {'dp','seq'}, use_global_device_ids=true, to_apply=%region_21.22.clone | all-reduce | flops 8192 | bytes 65536
  1790.1 33.7 %reduce-scatter.11.cloned.1.call-done = f32[128,1024]{1,0:T(8,128)} async-done(((f32[2048,1024]{1,0:T(8,128)}), f32[128,1024]{1,0:T(8,128)}) %reduce-scatter.11.cloned.1.call-update) | async-done | bytes 524304 | tf_op jit(solution)/shard_map/reduce_scatter | solution.py:252
  1823.8 107.6 %reduce-scatter.9.cloned.1.call-done = f32[128,1024]{1,0:T(8,128)} async-done(((f32[2048,1024]{1,0:T(8,128)}), f32[128,1024]{1,0:T(8,128)}) %reduce-scatter.9.cloned.1.call-update) | async-done | bytes 524304 | tf_op jit(solution)/shard_map/reduce_scatter | solution.py:251
  1931.4 181.6 %reduce-scatter.19.cloned.1.call-done = f32[128,2048]{1,0:T(8,128)} async-done(((f32[2048,2048]{1,0:T(8,128)}), f32[128,2048]{1,0:T(8,128)}) %reduce-scatter.19.cloned.1.call-update) | async-done | bytes 1048592 | tf_op jit(solution)/shard_map/reduce_scatter | solution.py:255
  2113.0 181.0 %reduce-scatter.21.cloned.1.call-done = f32[128,2048]{1,0:T(8,128)} async-done(((f32[2048,2048]{1,0:T(8,128)}), f32[128,2048]{1,0:T(8,128)}) %reduce-scatter.21.cloned.1.call-update) | async-done | bytes 1048592 | tf_op jit(solution)/shard_map/reduce_scatter | solution.py:256
  2294.0 180.8 %reduce-scatter.23.cloned.1.call-done = f32[2048,128]{1,0:T(8,128)} async-done(((f32[2048,2048]{1,0:T(8,128)}), f32[2048,128]{1,0:T(8,128)}) %reduce-scatter.23.cloned.1.call-update) | async-done | bytes 1048592 | tf_op jit(solution)/shard_map/reduce_scatter | solution.py:244
  2474.8 180.8 %reduce-scatter.17.cloned.1.call-done = f32[2048,128]{1,0:T(8,128)} async-done(((f32[2048,2048]{1,0:T(8,128)}), f32[2048,128]{1,0:T(8,128)}) %reduce-scatter.17.cloned.1.call-update) | async-done | bytes 1048592 | tf_op jit(solution)/shard_map/reduce_scatter | solution.py:243
  2655.6 181.2 %reduce-scatter.13.cloned.1.call-done = f32[128,2048]{1,0:T(8,128)} async-done(((f32[2048,2048]{1,0:T(8,128)}), f32[128,2048]{1,0:T(8,128)}) %reduce-scatter.13.cloned.1.call-update) | async-done | bytes 1048592 | tf_op jit(solution)/shard_map/reduce_scatter | solution.py:253
  2836.7 181.0 %reduce-scatter.15.cloned.1.call-done = f32[128,2048]{1,0:T(8,128)} async-done(((f32[2048,2048]{1,0:T(8,128)}), f32[128,2048]{1,0:T(8,128)}) %reduce-scatter.15.cloned.1.call-update) | async-done | bytes 1048592 | tf_op jit(solution)/shard_map/reduce_scatter | solution.py:254
  (277 shorter events, 274.3 us)
Async XLA Ops:
  7.2 68.7 %copy-start.4 = (bf16[2,256,2048]{2,1,0:T(8,128)(2,1)S(1)}, bf16[2,256,2048]{2,1,0:T(8,128)(2,1)}, u32[]{:S(2)}) copy-start(bf16[2,256,2048]{2,1,0:T(8,128)(2,1)} %param.19) | copy-start | bytes 6291460
  7.2 69.6 %copy-start.57 = (f32[4]{0:T(128)S(1)}, f32[4]{0:T(128)}, u32[]{:S(2)}) copy-start(f32[4]{0:T(128)} %param.32) | copy-start | bytes 52
  7.2 75.5 %all-gather.19.cloned.1.call-start = ((), (), s32[]{:S(2)}) async-start(), calls=%async_computation.11 | async-start | bytes 4456448 | tf_op jit(solution)/shard_map/all_gather | solution.py:91
  7.9 106.8 %all-gather.17.cloned.1.call-start = ((), (), s32[]{:S(2)}) async-start(), calls=%async_computation.10 | async-start | bytes 4456448 | tf_op jit(solution)/shard_map/all_gather | solution.py:90
  8.7 181.1 %all-gather.15.cloned.1.call-start = ((), (), s32[]{:S(2)}) async-start(), calls=%async_computation.9 | async-start | bytes 8912896 | tf_op jit(solution)/shard_map/all_gather | solution.py:92
  9.4 605.3 %all-gather.13.cloned.1.call-start = ((), (), s32[]{:S(2)}) async-start(), calls=%async_computation.8 | async-start | bytes 8912896 | tf_op jit(solution)/shard_map/all_gather | solution.py:93
  10.0 617.6 %all-gather.21.cloned.1.call-start = ((), (), s32[]{:S(2)}) async-start(), calls=%async_computation.12 | async-start | bytes 8912896 | tf_op jit(solution)/shard_map/all_gather | solution.py:103
  10.6 737.8 %all-reduce.10.cloned.1.call-start = ((), (), s32[]{:S(2)}) async-start(), calls=%async_computation.13 | async-start | bytes 8388608 | tf_op jit(solution)/shard_map/psum | solution.py:147
  44.8 35.7 %copy-start.42 = (f32[16,1,128]{2,1,0:T(1,128)}, f32[16,1,128]{2,1,0:T(1,128)S(1)}, u32[]{:S(2)}) copy-start(f32[16,1,128]{2,1,0:T(1,128)S(1)} %convert_element_type.159) | copy-start | bytes 24580
  76.9 127.4 %copy-start.44 = (f32[256,4]{0,1:T(4,128)}, f32[256,4]{0,1:T(4,128)S(1)}, u32[]{:S(2)}) copy-start(f32[256,4]{0,1:T(4,128)S(1)} %get-tuple-element.129) | copy-start | bytes 12292
  78.1 51.1 %copy-start.38 = (f32[256,128]{0,1:T(8,128)}, f32[256,128]{0,1:T(8,128)S(1)}, u32[]{:S(2)}) copy-start(f32[256,128]{0,1:T(8,128)S(1)} %get-tuple-element.127) | copy-start | bytes 393220
  78.3 51.6 %copy-start.10 = (f32[4,256,256]{2,1,0:T(8,128)}, f32[4,256,256]{2,1,0:T(8,128)S(1)}, u32[]{:S(2)}) copy-start(f32[4,256,256]{2,1,0:T(8,128)S(1)} %exponential_select_fusion) | copy-start | bytes 3145732
  214.2 374.2 %copy-start.20 = (bf16[2,256,4,128]{1,3,2,0:T(8,128)(2,1)S(1)}, bf16[2,256,4,128]{1,3,2,0:T(8,128)(2,1)}, u32[]{:S(2)}) copy-start(bf16[2,256,4,128]{1,3,2,0:T(8,128)(2,1)} %copy-done.19) | copy-start | bytes 1572868
  214.2 374.2 %copy-start.23 = (bf16[2,256,4,128]{1,3,2,0:T(8,128)(2,1)S(1)}, bf16[2,256,4,128]{1,3,2,0:T(8,128)(2,1)}, u32[]{:S(2)}) copy-start(bf16[2,256,4,128]{1,3,2,0:T(8,128)(2,1)} %copy-done.22) | copy-start | bytes 1572868
  214.2 159.7 %collective-permute-start = (f32[2,4,256,512]{3,2,1,0:T(8,128)}, f32[2,4,256,512]{3,2,1,0:T(8,128)}, u32[]{:S(2)}, u32[]{:S(2)}) collective-permute-start(f32[2,4,256,512]{3,2,1,0:T(8,128)} %get-tuple-element.204), channel_id=1, source_target_pairs={{0,1},{1,2},{2,3},{4,5},{5,6},{6,7},{8,9},{9,10},{10,11},{12,13},{... | collective-permute-start | bytes 12582920 | tf_op jit(solution)/shard_map/while/body/eval_jaxpr/ppermute | solution.py:15
  380.5 101.7 %collective-permute-start = (f32[2,4,256,512]{3,2,1,0:T(8,128)}, f32[2,4,256,512]{3,2,1,0:T(8,128)}, u32[]{:S(2)}, u32[]{:S(2)}) collective-permute-start(f32[2,4,256,512]{3,2,1,0:T(8,128)} %get-tuple-element.204), channel_id=1, source_target_pairs={{0,1},{1,2},{2,3},{4,5},{5,6},{6,7},{8,9},{9,10},{10,11},{12,13},{... | collective-permute-start | bytes 12582920 | tf_op jit(solution)/shard_map/while/body/eval_jaxpr/ppermute | solution.py:15
  488.8 93.0 %collective-permute-start = (f32[2,4,256,512]{3,2,1,0:T(8,128)}, f32[2,4,256,512]{3,2,1,0:T(8,128)}, u32[]{:S(2)}, u32[]{:S(2)}) collective-permute-start(f32[2,4,256,512]{3,2,1,0:T(8,128)} %get-tuple-element.204), channel_id=1, source_target_pairs={{0,1},{1,2},{2,3},{4,5},{5,6},{6,7},{8,9},{9,10},{10,11},{12,13},{... | collective-permute-start | bytes 12582920 | tf_op jit(solution)/shard_map/while/body/eval_jaxpr/ppermute | solution.py:15
  638.1 34.8 %copy-start.55 = (bf16[128]{0:T(256)(128)(2,1)S(1)}, bf16[128]{0:T(256)(128)(2,1)}, u32[]{:S(2)}) copy-start(bf16[128]{0:T(256)(128)(2,1)} %param.23) | copy-start | bytes 772
  638.2 186.7 %all-gather.23.cloned.1.call-start = ((), (), s32[]{:S(2)}) async-start(), calls=%async_computation.14 | async-start | bytes 8912896 | tf_op jit(solution)/shard_map/all_gather | solution.py:94
  638.9 261.1 %all-gather.25.cloned.1.call-start = ((), (), s32[]{:S(2)}) async-start(), calls=%async_computation.15 | async-start | bytes 8912896 | tf_op jit(solution)/shard_map/all_gather | solution.py:95
  639.7 338.8 %all-gather.27.cloned.1.call-start = ((), (), s32[]{:S(2)}) async-start(), calls=%async_computation.16 | async-start | bytes 8912896 | tf_op jit(solution)/shard_map/all_gather | solution.py:104
  640.4 472.0 %all-reduce.14.cloned.1.call-start = ((), (), s32[]{:S(2)}) async-start(), calls=%async_computation.18 | async-start | bytes 8388608 | tf_op jit(solution)/shard_map/psum | solution.py:170
  753.9 146.2 %copy-start.37 = (bf16[512,2048]{1,0:T(8,128)(2,1)}, bf16[512,2048]{1,0:T(8,128)(2,1)S(1)}, u32[]{:S(2)}) copy-start(bf16[512,2048]{1,0:T(8,128)(2,1)S(1)} %add_convert_fusion.2) | copy-start | bytes 6291460
  990.6 15.6 copy-start.59
  1006.1 172.1 %all-reduce.12.cloned.1.call-start = ((), (), s32[]{:S(2)}) async-start(), calls=%async_computation.17 | async-start | bytes 4194304 | tf_op jit(solution)/shard_map/psum | solution.py:155
  1015.5 699.1 %all-reduce.16.cloned.1.call-start = ((), (), s32[]{:S(2)}) async-start(), calls=%async_computation.19 | async-start | bytes 8388608 | tf_op jit(solution)/shard_map/psum | solution.py:237
  1185.0 13.5 copy-start.12
  1239.9 300.7 %copy-start.45 = (f32[256,4]{0,1:T(4,128)S(1)}, f32[256,4]{0,1:T(4,128)}, u32[]{:S(2)}) copy-start(f32[256,4]{0,1:T(4,128)} %copy-done.44) | copy-start | bytes 12292
  1239.9 94.5 %collective-permute-start.1 = (f32[2,4,256,512]{3,2,1,0:T(8,128)}, f32[2,4,256,512]{3,2,1,0:T(8,128)}, u32[]{:S(2)}, u32[]{:S(2)}) collective-permute-start(f32[2,4,256,512]{3,2,1,0:T(8,128)} %get-tuple-element.222), channel_id=1, source_target_pairs={{1,0},{2,1},{3,2},{5,4},{6,5},{7,6},{9,8},{10,9},{11,10},{13,12},{... | collective-permute-start | bytes 12582920 | tf_op jit(solution)/shard_map/while/body/eval_jaxpr/ppermute | solution.py:15
  1340.9 93.5 %collective-permute-start.1 = (f32[2,4,256,512]{3,2,1,0:T(8,128)}, f32[2,4,256,512]{3,2,1,0:T(8,128)}, u32[]{:S(2)}, u32[]{:S(2)}) collective-permute-start(f32[2,4,256,512]{3,2,1,0:T(8,128)} %get-tuple-element.222), channel_id=1, source_target_pairs={{1,0},{2,1},{3,2},{5,4},{6,5},{7,6},{9,8},{10,9},{11,10},{13,12},{... | collective-permute-start | bytes 12582920 | tf_op jit(solution)/shard_map/while/body/eval_jaxpr/ppermute | solution.py:15
  1441.0 92.6 %collective-permute-start.1 = (f32[2,4,256,512]{3,2,1,0:T(8,128)}, f32[2,4,256,512]{3,2,1,0:T(8,128)}, u32[]{:S(2)}, u32[]{:S(2)}) collective-permute-start(f32[2,4,256,512]{3,2,1,0:T(8,128)} %get-tuple-element.222), channel_id=1, source_target_pairs={{1,0},{2,1},{3,2},{5,4},{6,5},{7,6},{9,8},{10,9},{11,10},{13,12},{... | collective-permute-start | bytes 12582920 | tf_op jit(solution)/shard_map/while/body/eval_jaxpr/ppermute | solution.py:15
  1540.6 11.1 copy-start.27
  1577.7 12.4 copy-start.36
  1585.7 10.5 slice-start.2
  1607.4 216.3 %reduce-scatter.11.cloned.1.call-start = ((), (), s32[]{:S(2)}) async-start(), calls=%async_computation.21 | async-start | bytes 8912896 | tf_op jit(solution)/shard_map/reduce_scatter | solution.py:252
  1615.9 315.5 %reduce-scatter.9.cloned.1.call-start = ((), (), s32[]{:S(2)}) async-start(), calls=%async_computation.20 | async-start | bytes 8912896 | tf_op jit(solution)/shard_map/reduce_scatter | solution.py:251
  1621.9 491.1 %reduce-scatter.19.cloned.1.call-start = ((), (), s32[]{:S(2)}) async-start(), calls=%async_computation.25 | async-start | bytes 17825792 | tf_op jit(solution)/shard_map/reduce_scatter | solution.py:255
  1634.6 659.4 %reduce-scatter.21.cloned.1.call-start = ((), (), s32[]{:S(2)}) async-start(), calls=%async_computation.26 | async-start | bytes 17825792 | tf_op jit(solution)/shard_map/reduce_scatter | solution.py:256
  1647.2 827.6 %reduce-scatter.23.cloned.1.call-start = ((), (), s32[]{:S(2)}) async-start(), calls=%async_computation.27 | async-start | bytes 17825792 | tf_op jit(solution)/shard_map/reduce_scatter | solution.py:244
  1660.3 995.3 %reduce-scatter.17.cloned.1.call-start = ((), (), s32[]{:S(2)}) async-start(), calls=%async_computation.24 | async-start | bytes 17825792 | tf_op jit(solution)/shard_map/reduce_scatter | solution.py:243
  1673.8 1163.0 %reduce-scatter.13.cloned.1.call-start = ((), (), s32[]{:S(2)}) async-start(), calls=%async_computation.22 | async-start | bytes 17825792 | tf_op jit(solution)/shard_map/reduce_scatter | solution.py:253
  1684.0 1333.8 %reduce-scatter.15.cloned.1.call-start = ((), (), s32[]{:S(2)}) async-start(), calls=%async_computation.23 | async-start | bytes 17825792 | tf_op jit(solution)/shard_map/reduce_scatter | solution.py:254
  1695.5 19.1 copy-start.5
  1695.5 19.1 copy-start.43
  1695.6 19.1 copy-start.49
  1695.6 19.1 copy-start.51
  1695.6 22.7 copy-start.52
  1695.6 22.7 copy-start.53
  (44 other events, 214.2 us)
Sparse Core Ops, SparseCore 0:
  10.2 53.3 all-gather.18
  65.8 48.8 all-gather.16
  116.9 72.8 all-gather.14
  191.8 99.6 all-gather.12
  293.5 105.5 all-gather.20
  638.3 110.0 all-reduce.9
  750.6 74.2 all-gather.22
  827.1 72.8 all-gather.24
  902.1 76.2 all-gather.26
  1006.3 106.0 all-reduce.13
  1115.3 62.9 all-reduce.11
  1607.6 106.9 all-reduce.15
  1719.2 104.4 reduce-scatter.10
  1828.3 103.0 reduce-scatter.8
  1935.9 176.9 reduce-scatter.18
  2117.5 176.4 reduce-scatter.20
  2298.5 176.2 reduce-scatter.22
  2479.3 176.2 reduce-scatter.16
  2660.3 176.4 reduce-scatter.12
  2841.3 176.4 reduce-scatter.14
where the time goes:
time: 3030 us; the launch traced here: 3020 us
  waiting for transfers between devices  2350 us (78%)
  matrix products  271 us (9%)
  blocking collectives  188 us (6%)
  other arithmetic  92.2 us (3%)
  local copies, waits for them, and re-layouts  78.8 us (3%)
    ppermute x6, waiting for transfers between devices, passed_along(): return lax.ppermute(x, axis, pairs)  610 us
    reduce_scatter x1, waiting for transfers between devices, on_device(): lax.psum_scatter(grad_gate, ('dp', 'seq'), scatter_dimension=0, tiled=True)  182 us
    reduce_scatter x1, waiting for transfers between devices, on_device(): lax.psum_scatter(grad_wv, ('dp', 'seq'), scatter_dimension=0, tiled=True)  181 us
    reduce_scatter x1, waiting for transfers between devices, on_device(): lax.psum_scatter(grad_up, ('dp', 'seq'), scatter_dimension=0, tiled=True)  181 us
    reduce_scatter x1, waiting for transfers between devices, on_device(): lax.psum_scatter(grad_ws, ('dp', 'seq'), scatter_dimension=0, tiled=True)  181 us
    reduce_scatter x1, waiting for transfers between devices, on_device(): lax.psum_scatter(grad_out_w, ('dp', 'seq'), scatter_dimension=1, tiled=True)  181 us
    reduce_scatter x1, waiting for transfers between devices, on_device(): lax.psum_scatter(grad_down, ('dp', 'seq'), scatter_dimension=1, tiled=True)  181 us
    reduce_scatter x1, waiting for transfers between devices, on_device(): lax.psum_scatter(grad_wq, ('dp', 'seq'), scatter_dimension=0, tiled=True)  108 us
  transfers between devices with their start and end apart: 26, of which 23 were waited for; matrix products, arithmetic and copies ran while one was open for 8% of the time, Pallas kernels for 0%

commit v1 on v0

--- a/solution.py
+++ b/solution.py
@@ -7,6 +7,28 @@
 VH = 512
 eps = 1e-05
 highest_precision = lax.Precision.HIGHEST
+
+
+def order_samples_all_for(arr):
+    link_axis = ("dp", "seq")
+    heard = lax.axis_size(link_axis)
+    finding, reached, formed = (heard, lax.axis_index(link_axis), arr.shape[1])
+    earlier, carry_out = (arr, 1)
+    while carry_out < finding:
+        earlier = jnp.concatenate(
+            [
+                earlier,
+                lax.ppermute(
+                    earlier,
+                    axis_name=link_axis,
+                    perm=list(map(lambda d: (d, (d - carry_out) % finding), range(finding))),
+                ),
+            ],
+            axis=1,
+        )
+        carry_out = 2 * carry_out
+    near = jnp.roll(earlier, reached * formed, axis=1)
+    return near
 
 
 def passed_along(x, axis, by):
@@ -101,7 +123,7 @@
     query_full, key_full, value_full, swish_full, gate_full, up_full = gathered[4:]
     out_full, down_full = (
         lax.all_gather(w_out, ("dp", "seq"), axis=1, tiled=True),
-        lax.all_gather(w_down, ("dp", "seq"), axis=1, tiled=True),
+        order_samples_all_for(w_down),
     )
     seq_count, block, width = tokens.shape
     row_count = seq_count * block

time: 3030 us -> 2990 us (0.987)
  waiting for transfers between devices: 2350 us -> 2280 us
    ppermute x0 -> x4, waiting for transfers between devices: none -> 136 us  [order_samples_all_for(): lax.ppermute(earlier, axis_name=link_axis, perm=list(map(lambda d: (d, (d...]
    all_gather x1, waiting for transfers between devices: 71 us -> 0.02 us  [on_device(): lax.all_gather(w_gate, ('dp', 'seq'), axis=0, tiled=True)]
    all_gather x1 -> x0, waiting for transfers between devices: 69 us -> none  [on_device(): lax.all_gather(w_down, ('dp', 'seq'), axis=1, tiled=True)]
    psum x1, waiting for transfers between devices: 46.9 us -> 0.01 us  [on_device(): attention = lax.psum(matmul(mixed, out_full), 'tensor')]
  transfers between devices with their start and end apart: 26 -> 29, of which waited for: 23 -> 24; matrix products, arithmetic and copies ran while one was open for 8% -> 9% of each run, Pallas kernels for 0% -> 0%
where the time goes in v1:
time: 2990 us
  waiting for transfers between devices  2280 us (76%)
  matrix products  275 us (9%)
  blocking collectives  188 us (6%)
  local copies, waits for them, and re-layouts  99.2 us (3%)
  other arithmetic  97.1 us (3%)
  starting transfers between devices  33 us (1%)
    ppermute x6, waiting for transfers between devices, passed_along(): return lax.ppermute(x, axis, pairs)  609 us
    reduce_scatter x1, waiting for transfers between devices, on_device(): lax.psum_scatter(grad_gate, ('dp', 'seq'), scatter_dimension=0, tiled=True)  182 us
    reduce_scatter x1, waiting for transfers between devices, on_device(): lax.psum_scatter(grad_ws, ('dp', 'seq'), scatter_dimension=0, tiled=True)  181 us
    reduce_scatter x1, waiting for transfers between devices, on_device(): lax.psum_scatter(grad_wv, ('dp', 'seq'), scatter_dimension=0, tiled=True)  181 us
    reduce_scatter x1, waiting for transfers between devices, on_device(): lax.psum_scatter(grad_up, ('dp', 'seq'), scatter_dimension=0, tiled=True)  181 us
    reduce_scatter x1, waiting for transfers between devices, on_device(): lax.psum_scatter(grad_down, ('dp', 'seq'), scatter_dimension=1, tiled=True)  181 us
    reduce_scatter x1, waiting for transfers between devices, on_device(): lax.psum_scatter(grad_out_w, ('dp', 'seq'), scatter_dimension=1, tiled=True)  181 us
    ppermute x4, waiting for transfers between devices, order_samples_all_for(): lax.ppermute(earlier, axis_name=link_axis, perm=list(map(lambda d: (d, (d...  136 us
  transfers between devices with their start and end apart: 29, of which 24 were waited for; matrix products, arithmetic and copies ran while one was open for 9% of the time, Pallas kernels for 0%

profile of v1, /device:TPU:0, one launch (start us, length us, event | category | flops | bytes accessed | tf_op | source)
XLA Modules:
  0.0 2985.4 jit_solution(7609215481057859809)
XLA Ops:
  10.6 34.2 %all-gather = bf16[16,1,128]{2,1,0:T(2,128)(2,1)S(1)} all-gather(bf16[1,1,128]{2,1,0:T(2,128)(2,1)} %bitcast.200), channel_id=1, replica_groups=mesh['tensor'=2,'dp'=4,'seq'=4] {'dp','seq'}, dimensions={0}, use_global_device_ids=true | all-gather | bytes 4352 | tf_op jit(solution)/shard_map/all_gather | solution.py:108
  44.8 29.1 all-gather.1
  89.3 25.4 all-gather.16.cloned.1.call-done
  132.7 57.1 %all-gather.14.cloned.1.call-done = bf16[2048,2048]{1,0:T(8,128)(2,1)} async-done(((bf16[128,2048]{1,0:T(8,128)(2,1)}), bf16[2048,2048]{1,0:T(8,128)(2,1)}) %all-gather.14.cloned.1.call-update) | async-done | bytes 8388624 | tf_op jit(solution)/shard_map/all_gather | solution.py:114
  189.8 9.8 convolution_convert_fusion
  214.2 374.3 %while.24 = (s32[]{:T(128)}, f32[2,4,256,512]{3,2,1,0:T(8,128)}, f32[2,4,256,512]{3,2,1,0:T(8,128)}, f32[4]{0:T(128)S(1)}, f32[2,4,256,512]{3,2,1,0:T(8,128)}, /*index=5*/s32[]{:T(128)}) while((s32[]{:T(128)}, f32[2,4,256,512]{3,2,1,0:T(8,128)}, f32[2,4,256,512]{3,2,1,0:T(8,128)}, f32[4]{0:T(128)S(1)}, f32[2,4,256,512]{3,2,1,0:T(8,128)}, ...), condition=%wide.region_3.4_spmd, body=%wide.region_2.3_spmd.sunk | while | flops 2097154 | bytes 29360252 | solution.py:158
  219.7 154.2 %collective-permute-done = f32[2,4,256,512]{3,2,1,0:T(8,128)} collective-permute-done((f32[2,4,256,512]{3,2,1,0:T(8,128)}, f32[2,4,256,512]{3,2,1,0:T(8,128)}, u32[]{:S(2)}, u32[]{:S(2)}) %collective-permute-start) | collective-permute-done | bytes 4194336 | tf_op jit(solution)/shard_map/while/body/eval_jaxpr/ppermute | solution.py:37
  380.5 9.6 collective-permute-start
  390.1 92.1 %collective-permute-done = f32[2,4,256,512]{3,2,1,0:T(8,128)} collective-permute-done((f32[2,4,256,512]{3,2,1,0:T(8,128)}, f32[2,4,256,512]{3,2,1,0:T(8,128)}, u32[]{:S(2)}, u32[]{:S(2)}) %collective-permute-start) | collective-permute-done | bytes 4194336 | tf_op jit(solution)/shard_map/while/body/eval_jaxpr/ppermute | solution.py:37
  495.4 86.5 %collective-permute-done = f32[2,4,256,512]{3,2,1,0:T(8,128)} collective-permute-done((f32[2,4,256,512]{3,2,1,0:T(8,128)}, f32[2,4,256,512]{3,2,1,0:T(8,128)}, u32[]{:S(2)}, u32[]{:S(2)}) %collective-permute-start) | collective-permute-done | bytes 4194336 | tf_op jit(solution)/shard_map/while/body/eval_jaxpr/ppermute | solution.py:37
  615.1 12.8 multiply_convert_fusion.2
  627.8 10.5 fusion.72
  644.0 12.2 collective-permute-done.2
  656.4 48.5 %collective-permute-done.3 = bf16[2048,256]{1,0:T(8,128)(2,1)S(1)} collective-permute-done((bf16[2048,256]{1,0:T(8,128)(2,1)S(1)}, bf16[2048,256]{1,0:T(8,128)(2,1)S(1)}, u32[]{:S(2)}, u32[]{:S(2)}) %collective-permute-start.3) | collective-permute-done | bytes 1048608 | tf_op jit(solution)/shard_map/ppermute | solution.py:21
  706.3 23.5 collective-permute-done.4
  734.9 31.2 %all-gather.2 = bf16[16,1,128]{2,1,0:T(2,128)(2,1)S(1)} all-gather(bf16[1,1,128]{2,1,0:T(2,128)(2,1)S(1)} %bitcast.202), channel_id=1, replica_groups=mesh['tensor'=2,'dp'=4,'seq'=4] {'dp','seq'}, dimensions={0}, use_global_device_ids=true | all-gather | bytes 4352 | tf_op jit(solution)/shard_map/all_gather | solution.py:110
  766.2 29.3 all-gather.3
  802.2 52.2 %collective-permute-done.5 = bf16[2048,1024]{1,0:T(8,128)(2,1)} collective-permute-done((bf16[2048,1024]{1,0:T(8,128)(2,1)}, bf16[2048,1024]{1,0:T(8,128)(2,1)}, u32[]{:S(2)}, u32[]{:S(2)}) %collective-permute-start.5) | collective-permute-done | bytes 4194336 | tf_op jit(solution)/shard_map/ppermute | solution.py:21
  873.6 10.1 fusion.73
  883.7 42.2 %all-gather.24.cloned.1.call-done = bf16[2048,2048]{1,0:T(8,128)(2,1)} async-done(((bf16[128,2048]{1,0:T(8,128)(2,1)}), bf16[2048,2048]{1,0:T(8,128)(2,1)}) %all-gather.24.cloned.1.call-update) | async-done | bytes 8388624 | tf_op jit(solution)/shard_map/all_gather | solution.py:117
  925.9 9.6 fusion.74
  935.5 13.7 fusion.14
  966.8 9.3 fusion.35
  976.1 97.3 %all-reduce.14.cloned.1.call-done = f32[512,2048]{1,0:T(8,128)} async-done(((f32[512,2048]{1,0:T(8,128)}), f32[512,2048]{1,0:T(8,128)}) %all-reduce.14.cloned.1.call-update) | async-done | bytes 4194320 | tf_op jit(solution)/shard_map/psum | solution.py:192
  1078.4 60.7 %all-reduce.12.cloned.1.call-done = bf16[512,2048]{1,0:T(8,128)(2,1)} async-done(((bf16[512,2048]{1,0:T(8,128)(2,1)}), bf16[512,2048]{1,0:T(8,128)(2,1)}) %all-reduce.12.cloned.1.call-update) | async-done | bytes 2097168 | tf_op jit(solution)/shard_map/psum | solution.py:177
  1145.8 13.5 fusion.13
  1200.9 300.5 %while.25 = (s32[]{:T(128)}, f32[2,4,256,512]{3,2,1,0:T(8,128)}, f32[2,4,256,512]{3,2,1,0:T(8,128)}, f32[4]{0:T(128)S(1)}, f32[2,4,256,512]{3,2,1,0:T(8,128)}, /*index=5*/s32[]{:T(128)}) while((s32[]{:T(128)}, f32[2,4,256,512]{3,2,1,0:T(8,128)}, f32[2,4,256,512]{3,2,1,0:T(8,128)}, f32[4]{0:T(128)S(1)}, f32[2,4,256,512]{3,2,1,0:T(8,128)}, ...), condition=%wide.region_16.17_spmd, body=%wide.region_15.16_spmd.sunk | while | flops 2097154 | bytes 29360252 | solution.py:227
  1202.4 93.1 %collective-permute-done.1 = f32[2,4,256,512]{3,2,1,0:T(8,128)} collective-permute-done((f32[2,4,256,512]{3,2,1,0:T(8,128)}, f32[2,4,256,512]{3,2,1,0:T(8,128)}, u32[]{:S(2)}, u32[]{:S(2)}) %collective-permute-start.1) | collective-permute-done | bytes 4194336 | tf_op jit(solution)/shard_map/while/body/eval_jaxpr/ppermute | solution.py:37
  1303.3 92.2 %collective-permute-done.1 = f32[2,4,256,512]{3,2,1,0:T(8,128)} collective-permute-done((f32[2,4,256,512]{3,2,1,0:T(8,128)}, f32[2,4,256,512]{3,2,1,0:T(8,128)}, u32[]{:S(2)}, u32[]{:S(2)}) %collective-permute-start.1) | collective-permute-done | bytes 4194336 | tf_op jit(solution)/shard_map/while/body/eval_jaxpr/ppermute | solution.py:37
  1403.3 91.3 %collective-permute-done.1 = f32[2,4,256,512]{3,2,1,0:T(8,128)} collective-permute-done((f32[2,4,256,512]{3,2,1,0:T(8,128)}, f32[2,4,256,512]{3,2,1,0:T(8,128)}, u32[]{:S(2)}, u32[]{:S(2)}) %collective-permute-start.1) | collective-permute-done | bytes 4194336 | tf_op jit(solution)/shard_map/while/body/eval_jaxpr/ppermute | solution.py:37
  1501.4 11.1 fusion.46
  1557.1 11.2 add_add_fusion
  1583.0 12.6 fusion.83
  1595.7 12.5 fusion.84
  1608.5 12.6 fusion.85
  1621.2 13.4 fusion.53
  1634.7 10.1 fusion.81
  1646.4 10.0 fusion.82
  1658.3 17.2 all-reduce.16.cloned.1.call-done
  1679.1 63.9 %all-reduce.4 = (f32[2048]{0:T(1024)S(1)}, f32[2048]{0:T(1024)S(1)}, f32[2048]{0:T(1024)S(1)}, f32[2048]{0:T(1024)S(1)}) all-reduce(f32[2048]{0:T(1024)S(1)} %get-tuple-element.70, f32[2048]{0:T(1024)S(1)} %get-tuple-element.75, f32[2048]{0:T(1024)S(1)} %copy-done.61, ...), channel_id=2, replica_groups=mesh['tensor'=2,'dp'=4,'seq'=4] {'dp','seq'}, use_global_device_ids=true, to_apply=%region_21.22.clone | all-reduce | flops 8192 | bytes 65536
  1751.1 33.4 %reduce-scatter.11.cloned.1.call-done = f32[128,1024]{1,0:T(8,128)} async-done(((f32[2048,1024]{1,0:T(8,128)}), f32[128,1024]{1,0:T(8,128)}) %reduce-scatter.11.cloned.1.call-update) | async-done | bytes 524304 | tf_op jit(solution)/shard_map/reduce_scatter | solution.py:274
  1784.5 107.8 %reduce-scatter.9.cloned.1.call-done = f32[128,1024]{1,0:T(8,128)} async-done(((f32[2048,1024]{1,0:T(8,128)}), f32[128,1024]{1,0:T(8,128)}) %reduce-scatter.9.cloned.1.call-update) | async-done | bytes 524304 | tf_op jit(solution)/shard_map/reduce_scatter | solution.py:273
  1892.3 181.5 %reduce-scatter.19.cloned.1.call-done = f32[128,2048]{1,0:T(8,128)} async-done(((f32[2048,2048]{1,0:T(8,128)}), f32[128,2048]{1,0:T(8,128)}) %reduce-scatter.19.cloned.1.call-update) | async-done | bytes 1048592 | tf_op jit(solution)/shard_map/reduce_scatter | solution.py:277
  2073.8 181.0 %reduce-scatter.21.cloned.1.call-done = f32[128,2048]{1,0:T(8,128)} async-done(((f32[2048,2048]{1,0:T(8,128)}), f32[128,2048]{1,0:T(8,128)}) %reduce-scatter.21.cloned.1.call-update) | async-done | bytes 1048592 | tf_op jit(solution)/shard_map/reduce_scatter | solution.py:278
  2254.8 180.8 %reduce-scatter.23.cloned.1.call-done = f32[2048,128]{1,0:T(8,128)} async-done(((f32[2048,2048]{1,0:T(8,128)}), f32[2048,128]{1,0:T(8,128)}) %reduce-scatter.23.cloned.1.call-update) | async-done | bytes 1048592 | tf_op jit(solution)/shard_map/reduce_scatter | solution.py:266
  2435.6 180.8 %reduce-scatter.17.cloned.1.call-done = f32[2048,128]{1,0:T(8,128)} async-done(((f32[2048,2048]{1,0:T(8,128)}), f32[2048,128]{1,0:T(8,128)}) %reduce-scatter.17.cloned.1.call-update) | async-done | bytes 1048592 | tf_op jit(solution)/shard_map/reduce_scatter | solution.py:265
  2616.4 181.0 %reduce-scatter.13.cloned.1.call-done = f32[128,2048]{1,0:T(8,128)} async-done(((f32[2048,2048]{1,0:T(8,128)}), f32[128,2048]{1,0:T(8,128)}) %reduce-scatter.13.cloned.1.call-update) | async-done | bytes 1048592 | tf_op jit(solution)/shard_map/reduce_scatter | solution.py:275
  2797.5 181.1 %reduce-scatter.15.cloned.1.call-done = f32[128,2048]{1,0:T(8,128)} async-done(((f32[2048,2048]{1,0:T(8,128)}), f32[128,2048]{1,0:T(8,128)}) %reduce-scatter.15.cloned.1.call-update) | async-done | bytes 1048592 | tf_op jit(solution)/shard_map/reduce_scatter | solution.py:276
  (317 shorter events, 316.2 us)
Async XLA Ops:
  7.2 68.7 %copy-start.4 = (bf16[2,256,2048]{2,1,0:T(8,128)(2,1)S(1)}, bf16[2,256,2048]{2,1,0:T(8,128)(2,1)}, u32[]{:S(2)}) copy-start(bf16[2,256,2048]{2,1,0:T(8,128)(2,1)} %param.19) | copy-start | bytes 6291460
  7.2 69.6 %copy-start.65 = (f32[4]{0:T(128)S(1)}, f32[4]{0:T(128)}, u32[]{:S(2)}) copy-start(f32[4]{0:T(128)} %param.32) | copy-start | bytes 52
  7.2 75.4 %all-gather.18.cloned.1.call-start = ((), (), s32[]{:S(2)}) async-start(), calls=%async_computation.11 | async-start | bytes 4456448 | tf_op jit(solution)/shard_map/all_gather | solution.py:113
  7.9 106.8 %all-gather.16.cloned.1.call-start = ((), (), s32[]{:S(2)}) async-start(), calls=%async_computation.10 | async-start | bytes 4456448 | tf_op jit(solution)/shard_map/all_gather | solution.py:112
  8.7 181.1 %all-gather.14.cloned.1.call-start = ((), (), s32[]{:S(2)}) async-start(), calls=%async_computation.9 | async-start | bytes 8912896 | tf_op jit(solution)/shard_map/all_gather | solution.py:114
  9.4 605.7 %all-gather.12.cloned.1.call-start = ((), (), s32[]{:S(2)}) async-start(), calls=%async_computation.8 | async-start | bytes 8912896 | tf_op jit(solution)/shard_map/all_gather | solution.py:115
  10.0 617.8 %all-gather.20.cloned.1.call-start = ((), (), s32[]{:S(2)}) async-start(), calls=%async_computation.12 | async-start | bytes 8912896 | tf_op jit(solution)/shard_map/all_gather | solution.py:125
  10.6 857.3 %all-reduce.10.cloned.1.call-start = ((), (), s32[]{:S(2)}) async-start(), calls=%async_computation.13 | async-start | bytes 8388608 | tf_op jit(solution)/shard_map/psum | solution.py:169
  44.8 35.7 %copy-start.49 = (f32[16,1,128]{2,1,0:T(1,128)}, f32[16,1,128]{2,1,0:T(1,128)S(1)}, u32[]{:S(2)}) copy-start(f32[16,1,128]{2,1,0:T(1,128)S(1)} %convert_element_type.159) | copy-start | bytes 24580
  76.9 127.5 %copy-start.53 = (f32[256,4]{0,1:T(4,128)}, f32[256,4]{0,1:T(4,128)S(1)}, u32[]{:S(2)}) copy-start(f32[256,4]{0,1:T(4,128)S(1)} %get-tuple-element.129) | copy-start | bytes 12292
  76.9 511.6 %copy-start.51 = (f32[256,4]{0,1:T(4,128)}, f32[256,4]{0,1:T(4,128)S(1)}, u32[]{:S(2)}) copy-start(f32[256,4]{0,1:T(4,128)S(1)} %get-tuple-element.128) | copy-start | bytes 12292
  78.1 51.1 %copy-start.45 = (f32[256,128]{0,1:T(8,128)}, f32[256,128]{0,1:T(8,128)S(1)}, u32[]{:S(2)}) copy-start(f32[256,128]{0,1:T(8,128)S(1)} %get-tuple-element.127) | copy-start | bytes 393220
  78.3 51.6 %copy-start.10 = (f32[4,256,256]{2,1,0:T(8,128)}, f32[4,256,256]{2,1,0:T(8,128)S(1)}, u32[]{:S(2)}) copy-start(f32[4,256,256]{2,1,0:T(8,128)S(1)} %exponential_select_fusion) | copy-start | bytes 3145732
  214.2 374.3 %copy-start.26 = (bf16[2,256,4,128]{1,3,2,0:T(8,128)(2,1)S(1)}, bf16[2,256,4,128]{1,3,2,0:T(8,128)(2,1)}, u32[]{:S(2)}) copy-start(bf16[2,256,4,128]{1,3,2,0:T(8,128)(2,1)} %copy-done.25) | copy-start | bytes 1572868
  214.2 374.3 %copy-start.29 = (bf16[2,256,4,128]{1,3,2,0:T(8,128)(2,1)S(1)}, bf16[2,256,4,128]{1,3,2,0:T(8,128)(2,1)}, u32[]{:S(2)}) copy-start(bf16[2,256,4,128]{1,3,2,0:T(8,128)(2,1)} %copy-done.28) | copy-start | bytes 1572868
  214.2 159.7 %collective-permute-start = (f32[2,4,256,512]{3,2,1,0:T(8,128)}, f32[2,4,256,512]{3,2,1,0:T(8,128)}, u32[]{:S(2)}, u32[]{:S(2)}) collective-permute-start(f32[2,4,256,512]{3,2,1,0:T(8,128)} %get-tuple-element.204), channel_id=1, source_target_pairs={{0,1},{1,2},{2,3},{4,5},{5,6},{6,7},{8,9},{9,10},{10,11},{12,13},{... | collective-permute-start | bytes 12582920 | tf_op jit(solution)/shard_map/while/body/eval_jaxpr/ppermute | solution.py:37
  380.5 101.7 %collective-permute-start = (f32[2,4,256,512]{3,2,1,0:T(8,128)}, f32[2,4,256,512]{3,2,1,0:T(8,128)}, u32[]{:S(2)}, u32[]{:S(2)}) collective-permute-start(f32[2,4,256,512]{3,2,1,0:T(8,128)} %get-tuple-element.204), channel_id=1, source_target_pairs={{0,1},{1,2},{2,3},{4,5},{5,6},{6,7},{8,9},{9,10},{10,11},{12,13},{... | collective-permute-start | bytes 12582920 | tf_op jit(solution)/shard_map/while/body/eval_jaxpr/ppermute | solution.py:37
  488.9 93.0 %collective-permute-start = (f32[2,4,256,512]{3,2,1,0:T(8,128)}, f32[2,4,256,512]{3,2,1,0:T(8,128)}, u32[]{:S(2)}, u32[]{:S(2)}) collective-permute-start(f32[2,4,256,512]{3,2,1,0:T(8,128)} %get-tuple-element.204), channel_id=1, source_target_pairs={{0,1},{1,2},{2,3},{4,5},{5,6},{6,7},{8,9},{9,10},{10,11},{12,13},{... | collective-permute-start | bytes 12582920 | tf_op jit(solution)/shard_map/while/body/eval_jaxpr/ppermute | solution.py:37
  638.3 235.3 %all-gather.22.cloned.1.call-start = ((), (), s32[]{:S(2)}) async-start(), calls=%async_computation.14 | async-start | bytes 8912896 | tf_op jit(solution)/shard_map/all_gather | solution.py:116
  639.1 286.8 %all-gather.24.cloned.1.call-start = ((), (), s32[]{:S(2)}) async-start(), calls=%async_computation.15 | async-start | bytes 8912896 | tf_op jit(solution)/shard_map/all_gather | solution.py:117
  639.8 433.5 %all-reduce.14.cloned.1.call-start = ((), (), s32[]{:S(2)}) async-start(), calls=%async_computation.17 | async-start | bytes 8388608 | tf_op jit(solution)/shard_map/psum | solution.py:192
  639.9 16.3 collective-permute-start.2
  656.2 77.0 %copy-start.17 = (bf16[2048,128]{1,0:T(8,128)(2,1)}, bf16[2048,128]{1,0:T(8,128)(2,1)S(1)}, u32[]{:S(2)}) copy-start(bf16[2048,128]{1,0:T(8,128)(2,1)S(1)} %collective-permute-done.2) | copy-start | bytes 1572868
  656.4 48.5 %collective-permute-start.3 = (bf16[2048,256]{1,0:T(8,128)(2,1)S(1)}, bf16[2048,256]{1,0:T(8,128)(2,1)S(1)}, u32[]{:S(2)}, u32[]{:S(2)}) collective-permute-start(bf16[2048,256]{1,0:T(8,128)(2,1)S(1)} %pad_maximum_fusion.4), channel_id=1, source_target_pairs={{0,14},{1,15},{2,0},{3,1},{4,2},{5,3},{6,4},{7,5},{8,6},{9,7},{10,... | collective-permute-start | bytes 3145736 | tf_op jit(solution)/shard_map/ppermute | solution.py:21
  706.2 28.8 copy-start.63
  706.2 60.0 %copy-start.64 = (bf16[128]{0:T(256)(128)(2,1)S(1)}, bf16[128]{0:T(256)(128)(2,1)}, u32[]{:S(2)}) copy-start(bf16[128]{0:T(256)(128)(2,1)} %param.23) | copy-start | bytes 772
  706.2 23.6 collective-permute-start.4
  733.2 121.1 %collective-permute-start.5 = (bf16[2048,1024]{1,0:T(8,128)(2,1)}, bf16[2048,1024]{1,0:T(8,128)(2,1)}, u32[]{:S(2)}, u32[]{:S(2)}) collective-permute-start(bf16[2048,1024]{1,0:T(8,128)(2,1)} %pad_maximum_fusion), channel_id=1, source_target_pairs={{0,8},{1,9},{2,10},{3,11},{4,12},{5,13},{6,14},{7,15},{8,0},{9,1},... | collective-permute-start | bytes 12582920 | tf_op jit(solution)/shard_map/ppermute | solution.py:21
  802.2 56.8 %copy-start.16 = (bf16[2048,128]{1,0:T(8,128)(2,1)S(1)}, bf16[2048,128]{1,0:T(8,128)(2,1)}, u32[]{:S(2)}) copy-start(bf16[2048,128]{1,0:T(8,128)(2,1)} %param.31) | copy-start | bytes 1572868
  802.2 57.7 %copy-start.18 = (bf16[2048,128]{1,0:T(8,128)(2,1)S(1)}, bf16[2048,128]{1,0:T(8,128)(2,1)}, u32[]{:S(2)}) copy-start(bf16[2048,128]{1,0:T(8,128)(2,1)} %copy-done.17) | copy-start | bytes 1572868
  873.6 52.3 %copy-start.43 = (bf16[512,2048]{1,0:T(8,128)(2,1)}, bf16[512,2048]{1,0:T(8,128)(2,1)S(1)}, u32[]{:S(2)}) copy-start(bf16[512,2048]{1,0:T(8,128)(2,1)S(1)} %add_convert_fusion.2) | copy-start | bytes 6291460
  925.9 23.3 slice-start.4
  925.9 32.1 %slice-start.6 = ((s8[8388608]{0:T(1024)(128)(4,1)}), s8[4194304]{0:T(1024)(128)(4,1)S(1)}, s32[]{:S(2)}) async-start(s8[8388608]{0:T(1024)(128)(4,1)} %bitcast.210), calls=%async_computation.33 | async-start | bytes 8388608
  966.7 172.4 %all-reduce.12.cloned.1.call-start = ((), (), s32[]{:S(2)}) async-start(), calls=%async_computation.16 | async-start | bytes 4194304 | tf_op jit(solution)/shard_map/psum | solution.py:177
  976.1 699.4 %all-reduce.16.cloned.1.call-start = ((), (), s32[]{:S(2)}) async-start(), calls=%async_computation.18 | async-start | bytes 8388608 | tf_op jit(solution)/shard_map/psum | solution.py:259
  1200.9 300.5 %copy-start.54 = (f32[256,4]{0,1:T(4,128)S(1)}, f32[256,4]{0,1:T(4,128)}, u32[]{:S(2)}) copy-start(f32[256,4]{0,1:T(4,128)} %copy-done.53) | copy-start | bytes 12292
  1200.9 94.5 %collective-permute-start.1 = (f32[2,4,256,512]{3,2,1,0:T(8,128)}, f32[2,4,256,512]{3,2,1,0:T(8,128)}, u32[]{:S(2)}, u32[]{:S(2)}) collective-permute-start(f32[2,4,256,512]{3,2,1,0:T(8,128)} %get-tuple-element.222), channel_id=1, source_target_pairs={{1,0},{2,1},{3,2},{5,4},{6,5},{7,6},{9,8},{10,9},{11,10},{13,12},{... | collective-permute-start | bytes 12582920 | tf_op jit(solution)/shard_map/while/body/eval_jaxpr/ppermute | solution.py:37
  1302.0 93.5 %collective-permute-start.1 = (f32[2,4,256,512]{3,2,1,0:T(8,128)}, f32[2,4,256,512]{3,2,1,0:T(8,128)}, u32[]{:S(2)}, u32[]{:S(2)}) collective-permute-start(f32[2,4,256,512]{3,2,1,0:T(8,128)} %get-tuple-element.222), channel_id=1, source_target_pairs={{1,0},{2,1},{3,2},{5,4},{6,5},{7,6},{9,8},{10,9},{11,10},{13,12},{... | collective-permute-start | bytes 12582920 | tf_op jit(solution)/shard_map/while/body/eval_jaxpr/ppermute | solution.py:37
  1402.0 92.6 %collective-permute-start.1 = (f32[2,4,256,512]{3,2,1,0:T(8,128)}, f32[2,4,256,512]{3,2,1,0:T(8,128)}, u32[]{:S(2)}, u32[]{:S(2)}) collective-permute-start(f32[2,4,256,512]{3,2,1,0:T(8,128)} %get-tuple-element.222), channel_id=1, source_target_pairs={{1,0},{2,1},{3,2},{5,4},{6,5},{7,6},{9,8},{10,9},{11,10},{13,12},{... | collective-permute-start | bytes 12582920 | tf_op jit(solution)/shard_map/while/body/eval_jaxpr/ppermute | solution.py:37
  1568.3 216.2 %reduce-scatter.11.cloned.1.call-start = ((), (), s32[]{:S(2)}) async-start(), calls=%async_computation.20 | async-start | bytes 8912896 | tf_op jit(solution)/shard_map/reduce_scatter | solution.py:274
  1576.8 315.5 %reduce-scatter.9.cloned.1.call-start = ((), (), s32[]{:S(2)}) async-start(), calls=%async_computation.19 | async-start | bytes 8912896 | tf_op jit(solution)/shard_map/reduce_scatter | solution.py:273
  1583.0 490.8 %reduce-scatter.19.cloned.1.call-start = ((), (), s32[]{:S(2)}) async-start(), calls=%async_computation.24 | async-start | bytes 17825792 | tf_op jit(solution)/shard_map/reduce_scatter | solution.py:277
  1595.7 659.1 %reduce-scatter.21.cloned.1.call-start = ((), (), s32[]{:S(2)}) async-start(), calls=%async_computation.25 | async-start | bytes 17825792 | tf_op jit(solution)/shard_map/reduce_scatter | solution.py:278
  1608.3 827.3 %reduce-scatter.23.cloned.1.call-start = ((), (), s32[]{:S(2)}) async-start(), calls=%async_computation.26 | async-start | bytes 17825792 | tf_op jit(solution)/shard_map/reduce_scatter | solution.py:266
  1621.2 995.2 %reduce-scatter.17.cloned.1.call-start = ((), (), s32[]{:S(2)}) async-start(), calls=%async_computation.23 | async-start | bytes 17825792 | tf_op jit(solution)/shard_map/reduce_scatter | solution.py:265
  1634.7 1162.8 %reduce-scatter.13.cloned.1.call-start = ((), (), s32[]{:S(2)}) async-start(), calls=%async_computation.21 | async-start | bytes 17825792 | tf_op jit(solution)/shard_map/reduce_scatter | solution.py:275
  1644.8 1333.7 %reduce-scatter.15.cloned.1.call-start = ((), (), s32[]{:S(2)}) async-start(), calls=%async_computation.22 | async-start | bytes 17825792 | tf_op jit(solution)/shard_map/reduce_scatter | solution.py:276
  1656.5 22.7 copy-start.61
  (57 other events, 406.5 us)
Sparse Core Ops, SparseCore 0:
  10.2 53.3 all-gather.17
  65.8 48.8 all-gather.15
  116.9 72.8 all-gather.13
  191.8 99.6 all-gather.11
  293.5 105.5 all-gather.19
  638.5 110.0 all-reduce.9
  750.8 100.1 all-gather.21
  853.2 72.6 all-gather.23
  966.8 106.5 all-reduce.13
  1076.1 62.9 all-reduce.11
  1568.4 106.9 all-reduce.15
  1680.0 104.4 reduce-scatter.10
  1789.1 103.0 reduce-scatter.8
  1896.8 176.9 reduce-scatter.18
  2078.3 176.4 reduce-scatter.20
  2259.3 176.2 reduce-scatter.22
  2440.2 176.2 reduce-scatter.16
  2621.0 176.4 reduce-scatter.12
  2802.1 176.4 reduce-scatter.14
